TPU v7x, 32 devices: a whole 2x2x4 slice. The times are simulated.
32 devices in a mesh: seq: 8 (over y, x, core), mp: 4 (over z).
Axes of the slice: x: 2, y: 2, z: 4, core: 2. Of those that a mesh axis runs over, the one named last changes fastest.
Arguments:
- inputs: bfloat16 [8192, 4096], P('seq', 'mp'), may hold values from -6 to 6
- conv_weight: bfloat16 [4, 4096], P(None, 'mp'), may hold values from -3 to 3
- conv_bias: bfloat16 [4096], P('mp'), may hold values from -3 to 3
- doc_start: int32 [8192], P('seq'), may hold values from 0 to 8191, as said below
- counts: int32 [8], P('seq'), may hold values from 341 to 1024
Outputs:
- gram: float32 [4096, 4096], P('seq', 'mp')
Inputs may be any that keep to these rules, and one draw needn't show every extreme that they name: doc_start is never above the token's own position, and for t > 0 either doc_start[t] == t or doc_start[t] == doc_start[t - 1]; doc_start[0] is 0.
All inputs are finite; a program needn't handle non-finite values.
Results may differ from a plain program's by a relative error of at most 0.0003.
Values may be sent and summed in bfloat16 or wider, within the bound.
A program may use at most 64 MiB of HBM per device.

v0:
```python
import jax
import jax.numpy as jnp
from jax import lax
from jax.sharding import PartitionSpec as P


def passed_along(x, axis, by):
    peers = lax.axis_size(axis)
    pairs = [(i, i + by) for i in range(peers) if 0 <= i + by < peers]
    return lax.ppermute(x, axis, pairs)


def causal_conv(extended, weights, bias, position, doc_start, length):
    kernel_len = weights.shape[0]
    summed = jnp.zeros((length, weights.shape[1]), jnp.float32) + bias.astype(jnp.float32)
    for lag in range(kernel_len):
        window = extended[kernel_len - 1 - lag : kernel_len - 1 - lag + length].astype(jnp.float32)
        usable = position - lag >= doc_start
        summed = summed + jnp.where(usable[:, None], weights[lag].astype(jnp.float32) * window, 0.0)
    return jax.nn.silu(summed).astype(jnp.bfloat16)


def on_device(inputs, conv_weight, conv_bias, doc_start, counts):
    row_count = inputs.shape[0]
    kernel_len = conv_weight.shape[0]
    position = lax.axis_index("seq") * row_count + jnp.arange(row_count, dtype=jnp.int32)
    counted = jnp.arange(row_count, dtype=jnp.int32) < counts[0]
    token_total = lax.psum(counts.astype(jnp.float32)[0], "seq")
    prior = passed_along(inputs[row_count - (kernel_len - 1) :], "seq", 1)
    extended = jnp.concatenate([prior, inputs], axis=0)
    own_feats = causal_conv(extended, conv_weight, conv_bias, position, doc_start, row_count)
    kept = jnp.where(counted[:, None], own_feats, jnp.zeros_like(own_feats))
    whole = lax.all_gather(own_feats, "mp", axis=1, tiled=True)
    summed = lax.psum_scatter(
        lax.dot_general(whole, kept, (((0,), (0,)), ((), ())), preferred_element_type=jnp.float32),
        "seq",
        scatter_dimension=0,
        tiled=True,
    )
    return summed / token_total


def solution(mesh):
    placed = (P("seq", "mp"), P(None, "mp"), P("mp"), P("seq"), P("seq"))
    return jax.shard_map(
        on_device, mesh=mesh, in_specs=placed, out_specs=P("seq", "mp"), check_vma=False
    )
```

profile of v0, /device:TPU:6, one launch (start us, length us, event | category | flops | bytes accessed | tf_op | source)
XLA Modules:
  0.0 313.6 jit_solution(3767885994745322081)
XLA Ops:
  6.5 0.0 all-gather.2.cloned.1.call-start
  6.5 0.7 slice.26
  7.3 1.9 collective-permute-start
  9.2 0.9 slice_convert_fusion.3
  10.1 0.7 fusion.6
  10.8 0.7 convert_element_type.29
  11.4 0.8 collective-permute-done
  12.2 9.8 %multiply_convert_fusion = bf16[1024,1024]{1,0:T(8,128)(2,1)} fusion(bf16[1024,1024]{1,0:T(8,128)(2,1)} %param.5, bf16[3,1024]{1,0:T(4,128)(2,1)S(1)} %collective-permute-done, f32[1024]{0:T(1024)S(1)} %bitcast.10, f32[1024]{0:T(1024)S(1)} %bitcast.11, f32[1024]{0:T(1024)S(1)} %bitcast.9, f32[1024]{0:T(1024)S(1)} %bitcast.8, f32[1024]{0:T(1024)S(1)} %convert_element_type.29, ...), kind=kLoop, calls=%fused_computation | loop fusion | flops 31457280 | bytes 4225024 | tf_op jit(solution)/shard_map/convert_element_type | solution.py:20
  22.0 0.0 all-gather.2.cloned.1.call-update
  22.0 0.0 reduce-scatter.2.cloned.1.call-start
  22.7 150.2 %all-gather.2.cloned.1.call-done = bf16[1024,4096]{1,0:T(8,128)(2,1)} async-done(((bf16[1024,1024]{1,0:T(8,128)(2,1)}), bf16[1024,4096]{1,0:T(8,128)(2,1)}) %all-gather.2.cloned.1.call-update) | async-done | bytes 8388624 | tf_op jit(solution)/shard_map/all_gather | solution.py:33
  173.0 16.3 %fusion.2 = f32[4096,1024]{1,0:T(8,128)} fusion(bf16[1024,4096]{1,0:T(8,128)(2,1)} %all-gather.2.cloned.1.call-done, bf16[1024,1024]{1,0:T(8,128)(2,1)} %multiply_convert_fusion, pred[1024]{0:T(1024)(128)(4,1)S(1)} %iota_compare_fusion), kind=kOutput, calls=%fused_computation.6 | convolution fusion | flops 8590983168 | bytes 27264000 | tf_op jit(solution)/shard_map/dot_general | solution.py:35
  189.3 0.0 reduce-scatter.2.cloned.1.call-update
  189.3 11.5 %psum.7 = f32[]{:T(128)} all-reduce(f32[]{:T(128)} %bitcast.5), channel_id=1, replica_groups=mesh['seq'=8,'mp'=4] {'seq'}, use_global_device_ids=true, to_apply=%region_1.2 | all-reduce | flops 1 | bytes 8 | tf_op jit(solution)/shard_map/psum | solution.py:28
  200.8 102.1 %reduce-scatter.2.cloned.1.call-done = f32[512,1024]{1,0:T(8,128)} async-done(((f32[4096,1024]{1,0:T(8,128)}), f32[512,1024]{1,0:T(8,128)}) %reduce-scatter.2.cloned.1.call-update) | async-done | bytes 2097168 | tf_op jit(solution)/shard_map/reduce_scatter | solution.py:34
  302.9 3.8 %broadcast_divide_fusion = f32[512,1024]{1,0:T(8,128)} fusion(f32[512,1024]{1,0:T(8,128)} %reduce-scatter.2.cloned.1.call-done, f32[]{:T(128)} %psum.7), kind=kLoop, calls=%fused_computation.9 | loop fusion | flops 524288 | bytes 4194308 | tf_op jit(solution)/shard_map/div | solution.py:40
  (1 shorter events, 0.0 us)
Async XLA Ops:
  6.5 166.4 %all-gather.2.cloned.1.call-start = ((), (), s32[]{:S(2)}) async-start(), calls=%async_computation.1 | async-start | bytes 10485760 | tf_op jit(solution)/shard_map/all_gather | solution.py:33
  7.3 5.0 %collective-permute-start = (bf16[3,1024]{1,0:T(4,128)(2,1)S(1)}, bf16[3,1024]{1,0:T(4,128)(2,1)S(1)}, u32[]{:S(2)}, u32[]{:S(2)}) collective-permute-start(bf16[3,1024]{1,0:T(4,128)(2,1)S(1)} %slice.26), channel_id=1, source_target_pairs={{0,4},{4,8},{8,12},{12,16},{16,20},{20,24},{24,28},{1,5},{5,9},{9,... | collective-permute-start | bytes 18440 | tf_op jit(solution)/shard_map/ppermute | solution.py:10
  22.0 280.9 %reduce-scatter.2.cloned.1.call-start = ((), (), s32[]{:S(2)}) async-start(), calls=%async_computation.2 | async-start | bytes 18874368 | tf_op jit(solution)/shard_map/reduce_scatter | solution.py:34
Sparse Core Ops, SparseCore 0:
  22.1 150.7 all-gather.1
  189.4 113.4 reduce-scatter.1
where the time goes:
time: 316 us; the launch traced here: 314 us
  waiting for transfers between devices  253 us (80%)
  matrix products  16.3 us (5%)
  other arithmetic  15.8 us (5%)
  between operations  14.1 us (4%)
  blocking collectives  11.5 us (4%)
    all_gather x1, waiting for transfers between devices, on_device(): whole = lax.all_gather(own_feats, 'mp', axis=1, tiled=True)  150 us
    reduce_scatter x1, waiting for transfers between devices, on_device(): lax.psum_scatter(lax.dot_general(whole, kept, (((0,), (0,)), ((), ())), p...  102 us
    dot_general x1, matrix products, on_device(): lax.dot_general(whole, kept, (((0,), (0,)), ((), ())), preferred_element_...  16.3 us
    psum x1, blocking collectives, on_device(): token_total = lax.psum(counts.astype(jnp.float32)[0], 'seq')  11.5 us
    convert_element_type x1, other arithmetic, causal_conv(): return jax.nn.silu(summed).astype(jnp.bfloat16)  9.77 us
  transfers between devices with their start and end apart: 3, of which 3 were waited for; matrix products, arithmetic and copies ran while one was open for 1% of the time, Pallas kernels for 0%

commit v1 on v0

--- a/solution.py
+++ b/solution.py
@@ -1,7 +1,344 @@
+import functools
+
 import jax
 import jax.numpy as jnp
 from jax import lax
+from jax.experimental import pallas as pl
+from jax.experimental.pallas import tpu as pltpu
 from jax.sharding import PartitionSpec as P
+
+MESH = pl.DeviceIdType.MESH
+LANES = 128
+HALO = 16
+
+
+def when(cond):
+    return pl.when(cond)
+
+
+def gram_kernel(peers, depth, taps, x_hbm, taps_ref, code_ref, cnt_ref, o_ref, ext, feats, got, part,
+                from_x, from_y, sum_y, sum_x, totals,
+                load_sem, halo_sem, cnt_send, cnt_recv, pair_send, pair_recv,
+                up_send, down_send, fwd_send, got_recv,
+                a1_send, a1_recv, b1_send, b1_recv, a2_send, a2_recv, b2_send, b2_recv):
+    s, z = lax.axis_index("seq"), lax.axis_index("mp")
+    core, x, y = lax.rem(s, 2), lax.rem(s // 2, 2), s // 4
+    sib, over_x, over_y = s + 1 - 2 * core, s + 2 - 4 * x, s + 4 - 8 * y
+    quad = s // 2
+    rows, width = x_hbm.shape
+    half = width // 2
+    pieces = half // LANES
+
+    def remote(src, dst, send, recv, to):
+        return pltpu.make_async_remote_copy(src_ref=src, dst_ref=dst, send_sem=send, recv_sem=recv,
+                                            device_id=to, device_id_type=MESH)
+
+    load = pltpu.make_async_copy(x_hbm, ext.at[pl.ds(HALO, rows)], load_sem)
+    load.start()
+
+    barrier = pltpu.get_barrier_semaphore()
+    for step in range(1, peers):
+        pl.semaphore_signal(barrier, inc=1, device_id=(lax.rem(s + step, peers), z), device_id_type=MESH)
+
+    @when(z > 0)
+    def _():
+        pl.semaphore_signal(barrier, inc=1, device_id=(s, z - 1), device_id_type=MESH)
+
+    @when(z < depth - 1)
+    def _():
+        pl.semaphore_signal(barrier, inc=1, device_id=(s, z + 1), device_id_type=MESH)
+
+    pl.semaphore_wait(barrier, peers - 1 + jnp.where(z > 0, 1, 0) + jnp.where(z < depth - 1, 1, 0))
+
+    halo = remote(x_hbm.at[pl.ds(rows - HALO, HALO)], ext.at[pl.ds(0, HALO)], halo_sem.at[0], halo_sem.at[1],
+                  (lax.rem(s + 1, peers), z))
+
+    @when(s < peers - 1)
+    def _():
+        halo.start()
+
+    def cnt_copy(step, slot):
+        return remote(cnt_ref, totals.at[slot], cnt_send.at[step], cnt_recv.at[slot],
+                      (lax.rem(s + step, peers), z))
+
+    for step in range(1, peers):
+        cnt_copy(step, s).start()
+
+    load.wait()
+
+    @when(s == 0)
+    def _():
+        ext[0:HALO, :] = jnp.zeros((HALO, width), ext.dtype)
+
+    @when(s > 0)
+    def _():
+        halo.wait_recv()
+
+    block = LANES
+    own_rows = pl.multiple_of(core * rows, rows)
+
+    def conv(column):
+        at = pl.ds(pl.multiple_of(column, LANES), LANES)
+        taps_here = taps_ref[:, at]
+
+        def body(r, _):
+            first = pl.multiple_of(r * block, block)
+            seen = ext[pl.ds(first, block + HALO), at].astype(jnp.float32)
+            code = code_ref[pl.ds(first, block), :]
+            lags = jnp.bitwise_and(code, taps - 1)
+            total = jnp.broadcast_to(taps_here[taps : taps + 1], (block, LANES))
+            for lag in range(taps):
+                window = (pltpu.roll(seen, lag, 0) if lag else seen)[HALO:]
+                term = jnp.broadcast_to(taps_here[lag : lag + 1], (block, LANES)) * window
+                total = total + jnp.where(lags >= lag, term, 0.0)
+            value = total / (1.0 + jnp.exp(-total))
+            value = jnp.where(code >= taps, value, 0.0)
+            feats[pl.ds(pl.multiple_of(own_rows + first, block), block), at] = value.astype(feats.dtype)
+            return 0
+
+        lax.fori_loop(0, rows // block, body, 0)
+
+    def pair_copy(piece, row0):
+        spot = feats.at[pl.ds(row0, rows), pl.ds(pl.multiple_of(piece * LANES, LANES), LANES)]
+        return remote(spot, spot, pair_send.at[piece], pair_recv.at[piece], (sib, z))
+
+    def own_piece(k):
+        return feats.at[:, pl.ds(pl.multiple_of(core * half + k * LANES, LANES), LANES)]
+
+    def up_copy(k):
+        return remote(own_piece(k), got.at[z, k], up_send.at[k], got_recv.at[z, k], (s, lax.rem(z + 1, depth)))
+
+    def down_copy(k):
+        return remote(own_piece(k), got.at[z, k], down_send.at[k], got_recv.at[z, k],
+                      (s, lax.rem(z + depth - 1, depth)))
+
+    def spread(k, _):
+        for side in (1 - core, core):
+            piece = side * pieces + k
+            conv(piece * LANES)
+            pair_copy(piece, own_rows).start()
+        pair_copy(core * pieces + k, own_rows).wait_recv()
+
+        @when(z < depth - 1)
+        def _():
+            up_copy(k).start()
+
+        @when(z > 0)
+        def _():
+            down_copy(k).start()
+
+        return 0
+
+    lax.fori_loop(0, pieces, spread, 0)
+
+    def settle(k, _):
+        pair_copy((1 - core) * pieces + k, own_rows).wait_recv()
+        got[z, k] = feats[:, pl.ds(pl.multiple_of(core * half + k * LANES, LANES), LANES)]
+        return 0
+
+    lax.fori_loop(0, pieces, settle, 0)
+
+    steps = pieces + 2 * pieces * (depth - 1)
+
+    def place(i):
+        later = i - pieces
+        own = i < pieces
+        later = jnp.where(own, 0, later)
+        away = jnp.where(own, 0, later // (2 * pieces) + 1)
+        k = jnp.where(own, i, lax.rem(later, 2 * pieces) // 2)
+        sign = 1 - 2 * lax.rem(later, 2)
+        block_at = z + sign * away
+        valid = jnp.logical_and(block_at >= 0, block_at < depth)
+        block_in = jnp.where(valid, block_at, 0)
+        return away, k, sign, block_in, valid
+
+    def apart(block_at):
+        return lax.rem(block_at, 2) != x, block_at // 2 != y
+
+    def fwd_copy(block_at, k, sign):
+        to = lax.rem(z - sign + depth, depth)
+        return remote(got.at[block_at, k], got.at[block_at, k], fwd_send.at[block_at, k], got_recv.at[block_at, k],
+                      (s, to))
+
+    def a1_copy(b, k):
+        return remote(part.at[b, k, 0], from_x.at[b, k], a1_send.at[b, k], a1_recv.at[b, k], (over_x, z))
+
+    def b1_copy(b, k):
+        return remote(part.at[b, k, 1], from_y.at[b, k], b1_send.at[b, k], b1_recv.at[b, k], (over_y, z))
+
+    def a2_copy(b, k):
+        return remote(part.at[b, k, 0], sum_y.at[k], a2_send.at[b, k], a2_recv.at[k], (over_y, z))
+
+    def b2_copy(b, k):
+        return remote(part.at[b, k, 1], sum_x.at[k], b2_send.at[b, k], b2_recv.at[k], (over_x, z))
+
+    def product(i):
+        away, k, sign, b, valid = place(i)
+        beyond = z - sign
+        far_x, far_y = apart(b)
+
+        @when(valid)
+        def _():
+            @when(away > 0)
+            def _():
+                fwd_copy(b, k, sign).wait_recv()
+
+                @when(jnp.logical_and(beyond >= 0, beyond < depth))
+                def _():
+                    fwd_copy(b, k, sign).start()
+
+            for side in range(2):
+                part[b, k, side] = lax.dot_general(got[b, k], feats[:, side * half : (side + 1) * half],
+                                                   (((0,), (0,)), ((), ())), preferred_element_type=jnp.float32)
+
+            @when(far_x)
+            def _():
+                a1_copy(b, k).start()
+
+            @when(far_y)
+            def _():
+                b1_copy(b, k).start()
+
+    def combine(i):
+        _, k, _, b, valid = place(i)
+        far_x, far_y = apart(b)
+
+        @when(jnp.logical_and(valid, jnp.logical_and(jnp.logical_not(far_x), far_y)))
+        def _():
+            a1_copy(b, k).wait_recv()
+            part[b, k, 0] = part[b, k, 0] + from_x[b, k]
+            a2_copy(b, k).start()
+
+        @when(jnp.logical_and(valid, jnp.logical_and(far_x, jnp.logical_not(far_y))))
+        def _():
+            b1_copy(b, k).wait_recv()
+            part[b, k, 1] = part[b, k, 1] + from_y[b, k]
+            b2_copy(b, k).start()
+
+    lag = 2
+
+    def main(i, _):
+        @when(i < steps)
+        def _():
+            product(i)
+
+        @when(i >= lag)
+        def _():
+            combine(i - lag)
+
+        return 0
+
+    lax.fori_loop(0, steps + lag, main, 0)
+
+    for step in range(1, peers):
+        cnt_copy(step, lax.rem(s + peers - step, peers)).wait_recv()
+    totals[s] = cnt_ref[...]
+    token_total = jnp.sum(totals[...].astype(jnp.float32), axis=0)[0:1, :]
+    scale = jnp.broadcast_to(jnp.concatenate([1.0 / token_total] * (half // LANES), axis=1), (LANES, half))
+
+    def finish(k, _):
+        at = pl.ds(pl.multiple_of(k * LANES, LANES), LANES)
+        a1_copy(quad, k).wait_recv()
+        a2_copy(quad, k).wait_recv()
+        o_ref[at, 0:half] = (part[quad, k, 0] + from_x[quad, k] + sum_y[k]) * scale
+        b1_copy(quad, k).wait_recv()
+        b2_copy(quad, k).wait_recv()
+        o_ref[at, half : 2 * half] = (part[quad, k, 1] + from_y[quad, k] + sum_x[k]) * scale
+        return 0
+
+    lax.fori_loop(0, pieces, finish, 0)
+
+    @when(s < peers - 1)
+    def _():
+        halo.wait_send()
+
+    for step in range(1, peers):
+        cnt_copy(step, s).wait_send()
+
+    def sent(k, _):
+        for side in range(2):
+            pair_copy(side * pieces + k, own_rows).wait_send()
+
+        @when(z < depth - 1)
+        def _():
+            up_copy(k).wait_send()
+
+        @when(z > 0)
+        def _():
+            down_copy(k).wait_send()
+
+        return 0
+
+    lax.fori_loop(0, pieces, sent, 0)
+
+    def sent_late(i, _):
+        away, k, sign, b, valid = place(i)
+        beyond = z - sign
+        far_x, far_y = apart(b)
+
+        @when(jnp.logical_and(jnp.logical_and(valid, away > 0), jnp.logical_and(beyond >= 0, beyond < depth)))
+        def _():
+            fwd_copy(b, k, sign).wait_send()
+
+        @when(jnp.logical_and(valid, far_x))
+        def _():
+            a1_copy(b, k).wait_send()
+
+        @when(jnp.logical_and(valid, far_y))
+        def _():
+            b1_copy(b, k).wait_send()
+
+        @when(jnp.logical_and(valid, jnp.logical_and(jnp.logical_not(far_x), far_y)))
+        def _():
+            a2_copy(b, k).wait_send()
+
+        @when(jnp.logical_and(valid, jnp.logical_and(far_x, jnp.logical_not(far_y))))
+        def _():
+            b2_copy(b, k).wait_send()
+
+        return 0
+
+    lax.fori_loop(0, steps, sent_late, 0)
+
+
+def fused_on_device(peers, depth, inputs, conv_weight, conv_bias, doc_start, counts):
+    rows, width = inputs.shape
+    taps = conv_weight.shape[0]
+    half = width // 2
+    pieces = half // LANES
+    index = jnp.arange(rows, dtype=jnp.int32)
+    reach = jnp.minimum(lax.axis_index("seq") * rows + index - doc_start, taps - 1)
+    code = reach + jnp.where(index < counts[0], taps, 0)
+    code = jnp.broadcast_to(code[:, None], (rows, LANES))
+    cnt = jnp.broadcast_to(counts[0], (8, LANES))
+    taps_bias = jnp.concatenate([conv_weight, conv_bias[None]], axis=0).astype(jnp.float32)
+    vmem = pl.BlockSpec(memory_space=pltpu.VMEM)
+    dma = lambda *shape: pltpu.SemaphoreType.DMA(shape)
+    f32 = jnp.float32
+    grid = (depth, pieces)
+    return pl.pallas_call(
+        functools.partial(gram_kernel, peers, depth, taps),
+        out_shape=jax.ShapeDtypeStruct((half, width), f32),
+        in_specs=[pl.BlockSpec(memory_space=pl.ANY), vmem, vmem, vmem],
+        out_specs=vmem,
+        scratch_shapes=[
+            pltpu.VMEM((rows + HALO, width), inputs.dtype),
+            pltpu.VMEM((2 * rows, width), inputs.dtype),
+            pltpu.VMEM((depth, pieces, 2 * rows, LANES), inputs.dtype),
+            pltpu.VMEM((depth, pieces, 2, LANES, half), f32),
+            pltpu.VMEM((depth, pieces, LANES, half), f32),
+            pltpu.VMEM((depth, pieces, LANES, half), f32),
+            pltpu.VMEM((pieces, LANES, half), f32),
+            pltpu.VMEM((pieces, LANES, half), f32),
+            pltpu.VMEM((peers, 8, LANES), jnp.int32),
+            pltpu.SemaphoreType.DMA, dma(2), dma(peers), dma(peers), dma(2 * pieces), dma(2 * pieces),
+            dma(pieces), dma(pieces), dma(*grid), dma(*grid),
+            dma(*grid), dma(*grid), dma(*grid), dma(*grid), dma(*grid), dma(pieces), dma(*grid), dma(pieces),
+        ],
+        compiler_params=pltpu.CompilerParams(collective_id=0, has_side_effects=True,
+                                             vmem_limit_bytes=60 * 1024 * 1024),
+        name="gram",
+    )(inputs, taps_bias, code, cnt)
 
 
 def passed_along(x, axis, by):
@@ -42,6 +379,7 @@
 
 def solution(mesh):
     placed = (P("seq", "mp"), P(None, "mp"), P("mp"), P("seq"), P("seq"))
-    return jax.shard_map(
-        on_device, mesh=mesh, in_specs=placed, out_specs=P("seq", "mp"), check_vma=False
-    )
+    peers, depth = mesh.shape["seq"], mesh.shape["mp"]
+    fits = peers == 2 * depth and peers == 2**3
+    body = functools.partial(fused_on_device, peers, depth) if fits else on_device
+    return jax.shard_map(body, mesh=mesh, in_specs=placed, out_specs=P("seq", "mp"), check_vma=False)

time: 316 us -> 177 us (0.56)
  waiting for transfers between devices: 253 us -> 0 us
  Pallas kernels: 0 us -> 168 us
  matrix products: 16.3 us -> 0 us
  other arithmetic: 15.8 us -> 2 us
  between operations: 14.1 us -> 0.66 us
  blocking collectives: 11.5 us -> 0 us
  local copies, waits for them, and re-layouts: 0.72 us -> 5.43 us
    pallas_call x0 -> x1, Pallas kernels: none -> 168 us  [fused_on_device(): pl.pallas_call(functools.partial(gram_kernel, peers, depth, taps), out_sh...]
    all_gather x1 -> x0, waiting for transfers between devices: 150 us -> none  [on_device(): whole = lax.all_gather(own_feats, 'mp', axis=1, tiled=True)]
    reduce_scatter x1 -> x0, waiting for transfers between devices: 102 us -> none  [on_device(): lax.psum_scatter(lax.dot_general(whole, kept, (((0,), (0,)), ((), ())), p...]
    dot_general x1 -> x0, matrix products: 16.3 us -> none  [on_device(): lax.dot_general(whole, kept, (((0,), (0,)), ((), ())), preferred_element_...]
    psum x1 -> x0, blocking collectives: 11.5 us -> none  [on_device(): token_total = lax.psum(counts.astype(jnp.float32)[0], 'seq')]
    convert_element_type x2 -> x1, other arithmetic: 10.5 us -> 1.31 us  [fused_on_device(): jnp.concatenate([conv_weight, conv_bias[None]], axis=0).astype(jnp.float32)]
    div x1 -> x0, other arithmetic: 3.83 us -> none  [on_device(): return summed / token_total]
  transfers between devices with their start and end apart: 3 -> 0, of which waited for: 3 -> 0; matrix products, arithmetic and copies ran while one was open for 1% -> 0% of each run, Pallas kernels for 0% -> 0%
where the time goes in v1:
time: 177 us; the launch traced here: 176 us
  Pallas kernels  168 us (95%)
  local copies, waits for them, and re-layouts  5.43 us (3%)
  other arithmetic  2 us (1%)
    pallas_call x1, Pallas kernels, fused_on_device(): pl.pallas_call(functools.partial(gram_kernel, peers, depth, taps), out_sh...  168 us

profile of v1, /device:TPU:6, one launch (start us, length us, event | category | flops | bytes accessed | tf_op | source)
XLA Modules:
  0.0 176.3 jit_solution(2934907971771485169)
XLA Ops:
  0.7 0.7 select_add_fusion
  1.3 0.7 broadcast_in_dim.20
  2.0 0.6 broadcast_in_dim.24.cnt_ref
  2.6 1.3 maximum_convert_fusion.taps_ref
  3.9 1.0 broadcast_in_dim.23.code_ref
  4.9 168.2 %gram.1 = f32[512,1024]{1,0:T(8,128)} custom-call(bf16[1024,1024]{1,0:T(8,128)(2,1)} %x_hbm.1, f32[5,1024]{1,0:T(8,128)} %maximum_convert_fusion.taps_ref, s32[1024,128]{1,0:T(8,128)} %broadcast_in_dim.23.code_ref, s32[8,128]{1,0:T(8,128)} %broadcast_in_dim.24.cnt_ref), custom_call_target="tpu_custom_call" | custom-call | tf_op jit(solution)/shard_map/gram/pallas_call | solution.py:319
  173.2 3.2 %copy.8 = f32[512,1024]{1,0:T(8,128)} copy(f32[512,1024]{1,0:T(8,128)} %gram.1) | data formatting | bytes 4194304
